TPU v7x, 32 devices: a whole 2x2x4 slice. The times are simulated.
32 devices in a mesh: dp: 8 (over z, y), mp: 4 (over x, core).
Axes of the slice: x: 2, y: 2, z: 4, core: 2. Of those that a mesh axis runs over, the one named last changes fastest.
Arguments:
- hidden_input: bfloat16 [8192, 24], P('dp'), may hold values from -6 to 6
- output_cotangent: bfloat16 [8192, 8192], P('dp', 'mp'), may hold values from -0.023925781 to 0.023925781
- master_weights: float32 [24, 8192], P('dp', 'mp'), may hold values from -6 to 6
- first_codes: int32 [24, 8192], P('dp', 'mp'), may hold values from 0 to 15
- second_codes: int32 [24, 8192], P('dp', 'mp'), may hold values from 0 to 15
- first_rows: float32 [24], P('dp'), may hold values from 0.001 to 0.03
- first_cols: float32 [8192], P('mp'), may hold values from 0.001 to 0.03
- second_rows: float32 [24], P('dp'), may hold values from 1e-05 to 0.001
- second_cols: float32 [8192], P('mp'), may hold values from 1e-05 to 0.001
- step_count: int32 [], replicated, may hold values from 1 to 9
Outputs:
- new_master: float32 [24, 8192], P('dp', 'mp')
- update_ratio: float32 [24, 8192], P('dp', 'mp')
- gathered_params: bfloat16 [24, 8192], P(None, 'mp')
- first_scaled: float32 [24, 8192], P('dp', 'mp')
- second_scaled: float32 [24, 8192], P('dp', 'mp')
- new_first_rows: float32 [24], P('dp')
- new_first_cols: float32 [8192], P('mp')
- new_second_rows: float32 [24], P('dp')
- new_second_cols: float32 [8192], P('mp')
All inputs are finite; a program needn't handle non-finite values.
Results may differ from a plain program's by a relative error of at most 0.001.
Values may be sent and summed in bfloat16 or wider, within the bound.
A program may use at most 64 MiB of HBM per device.

v0:
```python
import jax
import jax.numpy as jnp
from jax import lax
from jax.sharding import PartitionSpec as P


def shards(
    hidden_input,
    output_cotangent,
    master_weights,
    first_codes,
    second_codes,
    first_rows,
    first_cols,
    second_rows,
    second_cols,
    step_count,
):
    local_rows = master_weights.shape[0]
    local_cols = master_weights.shape[1]
    whole_term = jnp.dot(hidden_input.T, output_cotangent, preferred_element_type=jnp.float32)
    column_share = lax.psum_scatter(whole_term, "dp", scatter_dimension=1, tiled=True)
    gradient = lax.all_to_all(column_share, "dp", split_axis=0, concat_axis=1, tiled=True)
    squares = lax.psum(jnp.sum(gradient * gradient), ("dp", "mp"))
    entries = local_rows * local_cols * lax.axis_size("dp") * lax.axis_size("mp")
    clipf = jnp.minimum(1.0, 0.01 * jnp.sqrt(jnp.float32(entries)) / (jnp.sqrt(squares) + 1e-06))
    clipped = clipf * gradient
    first_old = (
        (first_codes.astype(jnp.float32) - 7.5)
        / 7.5
        * jnp.minimum(first_rows[:, None], first_cols[None, :])
    )
    second_level = (second_codes.astype(jnp.float32) + 1.0) / 16.0
    second_old = (
        second_level * second_level * jnp.minimum(second_rows[:, None], second_cols[None, :])
    )
    first_new = 0.9 * first_old + 0.1 * clipped
    second_new = 0.95 * second_old + 0.05 * clipped * clipped
    steps = step_count.astype(jnp.float32)
    first_fix = 1.0 - jnp.power(jnp.float32(0.9), steps)
    second_fix = 1.0 - jnp.power(jnp.float32(0.95), steps)
    update_ratio = first_new / first_fix / (jnp.sqrt(second_new / second_fix) + 1e-08)
    new_master = master_weights - 0.001 * (update_ratio + 0.1 * master_weights)
    gathered_params = lax.all_gather(new_master.astype(jnp.bfloat16), "dp", axis=0, tiled=True)
    first_abs = jnp.abs(first_new)
    first_rowpart = jnp.max(first_abs, axis=1)
    first_colpart = jnp.max(first_abs, axis=0)
    second_rowpart = jnp.max(second_new, axis=1)
    second_colpart = jnp.max(second_new, axis=0)
    new_first_rows, new_second_rows = lax.pmax((first_rowpart, second_rowpart), "mp")
    new_first_cols, new_second_cols = lax.pmax((first_colpart, second_colpart), "dp")
    first_scaled = first_new / (
        jnp.minimum(new_first_rows[:, None], new_first_cols[None, :]) + 1e-08
    )
    second_scaled = second_new / (
        jnp.minimum(new_second_rows[:, None], new_second_cols[None, :]) + 1e-08
    )
    return (
        new_master,
        update_ratio,
        gathered_params,
        first_scaled,
        second_scaled,
        new_first_rows,
        new_first_cols,
        new_second_rows,
        new_second_cols,
    )


def solution(mesh):
    return jax.shard_map(
        shards,
        mesh=mesh,
        in_specs=(
            P("dp", None),
            P("dp", "mp"),
            P("dp", "mp"),
            P("dp", "mp"),
            P("dp", "mp"),
            P("dp"),
            P("mp"),
            P("dp"),
            P("mp"),
            P(),
        ),
        out_specs=(
            P("dp", "mp"),
            P("dp", "mp"),
            P(None, "mp"),
            P("dp", "mp"),
            P("dp", "mp"),
            P("dp"),
            P("mp"),
            P("dp"),
            P("mp"),
        ),
        check_vma=False,
    )
```

profile of v0, /device:TPU:0, one launch (start us, length us, event | category | flops | bytes accessed | tf_op | source)
XLA Modules:
  0.0 209.0 jit_solution(5620528497959128077)
XLA Ops:
  7.2 0.0 copy-start
  7.2 0.0 copy-start.4
  7.2 0.0 copy-start.8
  7.2 0.0 copy-start.5
  7.2 0.0 copy-start.9
  7.2 0.0 copy-start.1
  7.2 0.0 copy-start.2
  7.3 0.0 reduce-scatter.2.cloned.1.call-start
  7.3 0.7 copy-done
  8.0 3.5 %fusion.3 = f32[24,2048]{1,0:T(8,128)} fusion(bf16[1024,24]{0,1:T(8,128)(2,1)S(1)} %copy-done, bf16[1024,2048]{1,0:T(8,128)(2,1)} %param.11), kind=kOutput, calls=%fused_computation.13 | convolution fusion | flops 100663296 | bytes 4440064 | tf_op jit(solution)/shard_map/dot_general | solution.py:21
  11.5 0.0 reduce-scatter.2.cloned.1.call-update
  11.5 64.8 %reduce-scatter.2.cloned.1.call-done = f32[24,256]{1,0:T(8,128)} async-done(((f32[24,2048]{1,0:T(8,128)}), f32[24,256]{1,0:T(8,128)}) %reduce-scatter.2.cloned.1.call-update) | async-done | bytes 24592 | tf_op jit(solution)/shard_map/reduce_scatter | solution.py:22
  76.4 1.4 all_to_all.10
  77.7 3.6 %all-to-all-start = ((f32[8,3,256]{2,1,0:T(4,128)}), f32[8,3,256]{2,1,0:T(4,128)S(1)}, u32[]{:S(2)}, u32[]{:S(2)}) async-start(f32[8,3,256]{2,1,0:T(4,128)} %all_to_all.10), calls=%async_computation.1 | async-start | bytes 65536 | tf_op jit(solution)/shard_map/all_to_all | solution.py:23
  82.1 6.0 %all-to-all-done = f32[8,3,256]{2,1,0:T(4,128)S(1)} async-done(((f32[8,3,256]{2,1,0:T(4,128)}), f32[8,3,256]{2,1,0:T(4,128)S(1)}, u32[]{:S(2)}, u32[]{:S(2)}) %all-to-all-start) | async-done | bytes 24608 | tf_op jit(solution)/shard_map/all_to_all | solution.py:23
  88.0 0.6 multiply_reduce_fusion
  88.7 38.5 %psum.7 = f32[]{:T(128)} all-reduce(f32[]{:T(128)} %multiply_reduce_fusion), channel_id=1, replica_groups=mesh['dp'=8,'mp'=4] {'dp','mp'}, use_global_device_ids=true, to_apply=%region_2.0 | all-reduce | flops 1 | bytes 8 | tf_op jit(solution)/shard_map/psum | solution.py:24
  127.9 0.2 fusion.1
  128.2 6.5 %all-reduce.1 = (f32[3]{0:T(128)S(1)}, f32[3]{0:T(128)S(1)}) all-reduce(f32[3]{0:T(128)S(1)} %get-tuple-element.25, f32[3]{0:T(128)S(1)} %get-tuple-element.9), channel_id=1, replica_groups=mesh['dp'=8,'mp'=4] {'mp'}, use_global_device_ids=true, to_apply=%region_4.0 | all-reduce | flops 6 | bytes 48 | tf_op jit(solution)/shard_map/pmax | solution.py:50
  134.7 35.4 %all-reduce = (f32[2048]{0:T(1024)S(1)}, f32[2048]{0:T(1024)S(1)}) all-reduce(f32[2048]{0:T(1024)S(1)} %get-tuple-element.24, f32[2048]{0:T(1024)S(1)} %get-tuple-element.10), channel_id=1, replica_groups=mesh['dp'=8,'mp'=4] {'dp'}, use_global_device_ids=true, to_apply=%region_6.0 | all-reduce | flops 4096 | bytes 32768 | tf_op jit(solution)/shard_map/pmax | solution.py:51
  170.1 0.7 convert_bitcast_fusion
  170.9 30.5 %all-gather = bf16[8,3,2048]{2,1,0:T(4,128)(2,1)S(1)} all-gather(bf16[1,3,2048]{2,1,0:T(4,128)(2,1)S(1)} %get-tuple-element.19), channel_id=1, replica_groups=mesh['dp'=8,'mp'=4] {'dp'}, dimensions={0}, use_global_device_ids=true | all-gather | bytes 110592 | tf_op jit(solution)/shard_map/all_gather | solution.py:44
  201.4 0.7 reshape.32
  202.1 0.0 copy-done.10
  (16 shorter events, 0.0 us)
Async XLA Ops:
  7.2 0.8 copy-start
  7.2 120.7 %copy-start.4 = (f32[2048]{0:T(1024)S(1)}, f32[2048]{0:T(1024)}, u32[]{:S(2)}) copy-start(f32[2048]{0:T(1024)} %param.18) | copy-start | bytes 24580
  7.2 120.7 %copy-start.8 = (f32[3]{0:T(128)S(1)}, f32[3]{0:T(128)}, u32[]{:S(2)}) copy-start(f32[3]{0:T(128)} %param.17) | copy-start | bytes 40
  7.2 120.7 %copy-start.5 = (f32[2048]{0:T(1024)S(1)}, f32[2048]{0:T(1024)}, u32[]{:S(2)}) copy-start(f32[2048]{0:T(1024)} %param.16) | copy-start | bytes 24580
  7.2 120.7 %copy-start.9 = (f32[3]{0:T(128)S(1)}, f32[3]{0:T(128)}, u32[]{:S(2)}) copy-start(f32[3]{0:T(128)} %param.15) | copy-start | bytes 40
  7.2 120.7 %copy-start.1 = (s32[3,2048]{1,0:T(4,128)S(1)}, s32[3,2048]{1,0:T(4,128)}, u32[]{:S(2)}) copy-start(s32[3,2048]{1,0:T(4,128)} %param.14) | copy-start | bytes 73732
  7.2 120.7 %copy-start.2 = (s32[3,2048]{1,0:T(4,128)S(1)}, s32[3,2048]{1,0:T(4,128)}, u32[]{:S(2)}) copy-start(s32[3,2048]{1,0:T(4,128)} %param.13) | copy-start | bytes 73732
  7.3 162.9 %copy-start.3 = (f32[3,2048]{1,0:T(4,128)S(1)}, f32[3,2048]{1,0:T(4,128)}, u32[]{:S(2)}) copy-start(f32[3,2048]{1,0:T(4,128)} %param.12) | copy-start | bytes 73732
  7.3 69.1 %reduce-scatter.2.cloned.1.call-start = ((), (), s32[]{:S(2)}) async-start(), calls=%async_computation.2 | async-start | bytes 221184 | tf_op jit(solution)/shard_map/reduce_scatter | solution.py:22
  77.7 10.3 %all-to-all-start = ((f32[8,3,256]{2,1,0:T(4,128)}), f32[8,3,256]{2,1,0:T(4,128)S(1)}, u32[]{:S(2)}, u32[]{:S(2)}) async-start(f32[8,3,256]{2,1,0:T(4,128)} %all_to_all.10), calls=%async_computation.1 | async-start | bytes 65536 | tf_op jit(solution)/shard_map/all_to_all | solution.py:23
  134.7 67.4 %copy-start.10 = (f32[3]{0:T(128)}, f32[3]{0:T(128)S(1)}, u32[]{:S(2)}) copy-start(f32[3]{0:T(128)S(1)} %get-tuple-element.15) | copy-start | bytes 40
  134.7 67.4 %copy-start.11 = (f32[3]{0:T(128)}, f32[3]{0:T(128)S(1)}, u32[]{:S(2)}) copy-start(f32[3]{0:T(128)S(1)} %get-tuple-element.16) | copy-start | bytes 40
  170.1 32.0 %copy-start.6 = (f32[2048]{0:T(1024)}, f32[2048]{0:T(1024)S(1)}, u32[]{:S(2)}) copy-start(f32[2048]{0:T(1024)S(1)} %get-tuple-element.13) | copy-start | bytes 24580
  170.1 32.0 %copy-start.7 = (f32[2048]{0:T(1024)}, f32[2048]{0:T(1024)S(1)}, u32[]{:S(2)}) copy-start(f32[2048]{0:T(1024)S(1)} %get-tuple-element.14) | copy-start | bytes 24580
Sparse Core Ops, SparseCore 0:
  11.7 64.6 reduce-scatter.1
where the time goes:
time: 209 us
  blocking collectives  111 us (53%)
  waiting for transfers between devices  70.8 us (34%)
  between operations  15.7 us (8%)
  starting transfers between devices  3.65 us (2%)
  matrix products  3.52 us (2%)
  local copies, waits for them, and re-layouts  2.81 us (1%)
    reduce_scatter x1, waiting for transfers between devices, shards(): lax.psum_scatter(whole_term, 'dp', scatter_dimension=1, tiled=True)  64.8 us
    psum x1, blocking collectives, shards(): squares = lax.psum(jnp.sum(gradient * gradient), ('dp', 'mp'))  38.5 us
    pmax x1, blocking collectives, shards(): lax.pmax((first_colpart, second_colpart), 'dp')  35.4 us
    all_gather x1, blocking collectives, shards(): lax.all_gather(new_master.astype(jnp.bfloat16), 'dp', axis=0, tiled=True)  30.5 us
    pmax x1, blocking collectives, shards(): lax.pmax((first_rowpart, second_rowpart), 'mp')  6.54 us
    all_to_all x1, waiting for transfers between devices, shards(): lax.all_to_all(column_share, 'dp', split_axis=0, concat_axis=1, tiled=True)  5.95 us
  transfers between devices with their start and end apart: 2, of which 2 were waited for; matrix products, arithmetic and copies ran while one was open for 0% of the time, Pallas kernels for 0%

commit v1 on v0

--- a/solution.py
+++ b/solution.py
@@ -16,11 +16,21 @@
     second_cols,
     step_count,
 ):
+
+    def choose_bench(local_array, mesh_ax):
+        d_next = jnp.concatenate(
+            lax.all_to_all(
+                jnp.stack(jnp.split(local_array, lax.axis_size(mesh_ax), 0), axis=0), mesh_ax, 0, 0
+            ),
+            1,
+        )
+        return d_next
+
     local_rows = master_weights.shape[0]
     local_cols = master_weights.shape[1]
     whole_term = jnp.dot(hidden_input.T, output_cotangent, preferred_element_type=jnp.float32)
     column_share = lax.psum_scatter(whole_term, "dp", scatter_dimension=1, tiled=True)
-    gradient = lax.all_to_all(column_share, "dp", split_axis=0, concat_axis=1, tiled=True)
+    gradient = choose_bench(column_share, "dp")
     squares = lax.psum(jnp.sum(gradient * gradient), ("dp", "mp"))
     entries = local_rows * local_cols * lax.axis_size("dp") * lax.axis_size("mp")
     clipf = jnp.minimum(1.0, 0.01 * jnp.sqrt(jnp.float32(entries)) / (jnp.sqrt(squares) + 1e-06))

time: 209 us -> 219 us (1.048)
  local copies, waits for them, and re-layouts: 2.81 us -> 11.8 us
    unnamed x25 -> x32, local copies, waits for them, and re-layouts: 1.45 us -> 10.5 us
where the time goes in v1:
time: 219 us; the launch traced here: 218 us
  blocking collectives  111 us (51%)
  waiting for transfers between devices  70.8 us (32%)
  between operations  15.7 us (7%)
  local copies, waits for them, and re-layouts  11.8 us (5%)
  starting transfers between devices  3.65 us (2%)
  matrix products  3.52 us (2%)
    reduce_scatter x1, waiting for transfers between devices, shards(): lax.psum_scatter(whole_term, 'dp', scatter_dimension=1, tiled=True)  64.8 us
    psum x1, blocking collectives, shards(): squares = lax.psum(jnp.sum(gradient * gradient), ('dp', 'mp'))  38.5 us
    pmax x1, blocking collectives, shards(): lax.pmax((first_colpart, second_colpart), 'dp')  35.4 us
    all_gather x1, blocking collectives, shards(): lax.all_gather(new_master.astype(jnp.bfloat16), 'dp', axis=0, tiled=True)  30.5 us
    unnamed x32, local copies, waits for them, and re-layouts  10.5 us
    pmax x1, blocking collectives, shards(): lax.pmax((first_rowpart, second_rowpart), 'mp')  6.54 us
    all_to_all x1, waiting for transfers between devices, choose_bench(): lax.all_to_all(jnp.stack(jnp.split(local_array, lax.axis_size(mesh_ax), 0...  5.95 us
  transfers between devices with their start and end apart: 2, of which 2 were waited for; matrix products, arithmetic and copies ran while one was open for 0% of the time, Pallas kernels for 0%

profile of v1, /device:TPU:0, one launch (start us, length us, event | category | flops | bytes accessed | tf_op | source)
XLA Modules:
  0.0 218.0 jit_solution(5725910481369507343)
XLA Ops:
  7.2 0.0 copy-start
  7.3 0.0 reduce-scatter.2.cloned.1.call-start
  7.3 0.7 copy-done
  8.0 3.5 %fusion.3 = f32[24,2048]{1,0:T(8,128)} fusion(bf16[1024,24]{0,1:T(8,128)(2,1)S(1)} %copy-done, bf16[1024,2048]{1,0:T(8,128)(2,1)} %param.11), kind=kOutput, calls=%fused_computation.29 | convolution fusion | flops 100663296 | bytes 4440064 | tf_op jit(solution)/shard_map/dot_general | solution.py:31
  11.5 0.0 reduce-scatter.2.cloned.1.call-update
  11.5 64.8 %reduce-scatter.2.cloned.1.call-done = f32[24,256]{1,0:T(8,128)} async-done(((f32[24,2048]{1,0:T(8,128)}), f32[24,256]{1,0:T(8,128)}) %reduce-scatter.2.cloned.1.call-update) | async-done | bytes 24592 | tf_op jit(solution)/shard_map/reduce_scatter | solution.py:32
  76.4 1.3 constant_dynamic-update-slice_fusion.7
  77.7 1.3 constant_dynamic-update-slice_fusion.6
  79.0 1.3 constant_dynamic-update-slice_fusion.5
  80.3 1.3 constant_dynamic-update-slice_fusion.4
  81.6 1.3 constant_dynamic-update-slice_fusion.3
  82.9 1.3 constant_dynamic-update-slice_fusion.2
  84.2 1.3 constant_dynamic-update-slice_fusion.1
  85.5 1.3 constant_dynamic-update-slice_fusion
  86.7 3.6 %all-to-all-start = ((f32[8,3,256]{2,1,0:T(4,128)}), f32[8,3,256]{2,1,0:T(4,128)S(1)}, u32[]{:S(2)}, u32[]{:S(2)}) async-start(f32[8,3,256]{2,1,0:T(4,128)} %constant_dynamic-update-slice_fusion), calls=%async_computation.1 | async-start | bytes 65536 | tf_op jit(solution)/shard_map/all_to_all | solution.py:22
  91.1 6.0 %all-to-all-done = f32[8,3,256]{2,1,0:T(4,128)S(1)} async-done(((f32[8,3,256]{2,1,0:T(4,128)}), f32[8,3,256]{2,1,0:T(4,128)S(1)}, u32[]{:S(2)}, u32[]{:S(2)}) %all-to-all-start) | async-done | bytes 24608 | tf_op jit(solution)/shard_map/all_to_all | solution.py:22
  97.0 0.6 multiply_reduce_fusion
  97.7 38.5 %psum.7 = f32[]{:T(128)} all-reduce(f32[]{:T(128)} %multiply_reduce_fusion), channel_id=1, replica_groups=mesh['dp'=8,'mp'=4] {'dp','mp'}, use_global_device_ids=true, to_apply=%region_2.0 | all-reduce | flops 1 | bytes 8 | tf_op jit(solution)/shard_map/psum | solution.py:34
  136.9 0.2 fusion.1
  137.2 6.5 %all-reduce.1 = (f32[3]{0:T(128)S(1)}, f32[3]{0:T(128)S(1)}) all-reduce(f32[3]{0:T(128)S(1)} %get-tuple-element.25, f32[3]{0:T(128)S(1)} %get-tuple-element.9), channel_id=1, replica_groups=mesh['dp'=8,'mp'=4] {'mp'}, use_global_device_ids=true, to_apply=%region_4.0 | all-reduce | flops 6 | bytes 48 | tf_op jit(solution)/shard_map/pmax | solution.py:60
  143.7 35.4 %all-reduce = (f32[2048]{0:T(1024)S(1)}, f32[2048]{0:T(1024)S(1)}) all-reduce(f32[2048]{0:T(1024)S(1)} %get-tuple-element.24, f32[2048]{0:T(1024)S(1)} %get-tuple-element.10), channel_id=1, replica_groups=mesh['dp'=8,'mp'=4] {'dp'}, use_global_device_ids=true, to_apply=%region_6.0 | all-reduce | flops 4096 | bytes 32768 | tf_op jit(solution)/shard_map/pmax | solution.py:61
  179.1 0.7 convert_bitcast_fusion
  179.9 30.5 %all-gather = bf16[8,3,2048]{2,1,0:T(4,128)(2,1)S(1)} all-gather(bf16[1,3,2048]{2,1,0:T(4,128)(2,1)S(1)} %get-tuple-element.19), channel_id=1, replica_groups=mesh['dp'=8,'mp'=4] {'dp'}, dimensions={0}, use_global_device_ids=true | all-gather | bytes 110592 | tf_op jit(solution)/shard_map/all_gather | solution.py:54
  210.4 0.7 reshape.31
  (23 shorter events, 0.1 us)
Async XLA Ops:
  7.2 0.8 copy-start
  7.2 129.7 %copy-start.4 = (f32[2048]{0:T(1024)S(1)}, f32[2048]{0:T(1024)}, u32[]{:S(2)}) copy-start(f32[2048]{0:T(1024)} %param.18) | copy-start | bytes 24580
  7.2 129.7 %copy-start.8 = (f32[3]{0:T(128)S(1)}, f32[3]{0:T(128)}, u32[]{:S(2)}) copy-start(f32[3]{0:T(128)} %param.17) | copy-start | bytes 40
  7.2 129.7 %copy-start.5 = (f32[2048]{0:T(1024)S(1)}, f32[2048]{0:T(1024)}, u32[]{:S(2)}) copy-start(f32[2048]{0:T(1024)} %param.16) | copy-start | bytes 24580
  7.2 129.7 %copy-start.9 = (f32[3]{0:T(128)S(1)}, f32[3]{0:T(128)}, u32[]{:S(2)}) copy-start(f32[3]{0:T(128)} %param.15) | copy-start | bytes 40
  7.2 129.7 %copy-start.1 = (s32[3,2048]{1,0:T(4,128)S(1)}, s32[3,2048]{1,0:T(4,128)}, u32[]{:S(2)}) copy-start(s32[3,2048]{1,0:T(4,128)} %param.14) | copy-start | bytes 73732
  7.2 129.7 %copy-start.2 = (s32[3,2048]{1,0:T(4,128)S(1)}, s32[3,2048]{1,0:T(4,128)}, u32[]{:S(2)}) copy-start(s32[3,2048]{1,0:T(4,128)} %param.13) | copy-start | bytes 73732
  7.3 171.9 %copy-start.3 = (f32[3,2048]{1,0:T(4,128)S(1)}, f32[3,2048]{1,0:T(4,128)}, u32[]{:S(2)}) copy-start(f32[3,2048]{1,0:T(4,128)} %param.12) | copy-start | bytes 73732
  7.3 69.1 %reduce-scatter.2.cloned.1.call-start = ((), (), s32[]{:S(2)}) async-start(), calls=%async_computation.2 | async-start | bytes 221184 | tf_op jit(solution)/shard_map/reduce_scatter | solution.py:32
  86.7 10.3 %all-to-all-start = ((f32[8,3,256]{2,1,0:T(4,128)}), f32[8,3,256]{2,1,0:T(4,128)S(1)}, u32[]{:S(2)}, u32[]{:S(2)}) async-start(f32[8,3,256]{2,1,0:T(4,128)} %constant_dynamic-update-slice_fusion), calls=%async_computation.1 | async-start | bytes 65536 | tf_op jit(solution)/shard_map/all_to_all | solution.py:22
  143.7 67.4 %copy-start.10 = (f32[3]{0:T(128)}, f32[3]{0:T(128)S(1)}, u32[]{:S(2)}) copy-start(f32[3]{0:T(128)S(1)} %get-tuple-element.15) | copy-start | bytes 40
  143.7 67.4 %copy-start.11 = (f32[3]{0:T(128)}, f32[3]{0:T(128)S(1)}, u32[]{:S(2)}) copy-start(f32[3]{0:T(128)S(1)} %get-tuple-element.16) | copy-start | bytes 40
  179.1 32.0 %copy-start.6 = (f32[2048]{0:T(1024)}, f32[2048]{0:T(1024)S(1)}, u32[]{:S(2)}) copy-start(f32[2048]{0:T(1024)S(1)} %get-tuple-element.13) | copy-start | bytes 24580
  179.1 32.0 %copy-start.7 = (f32[2048]{0:T(1024)}, f32[2048]{0:T(1024)S(1)}, u32[]{:S(2)}) copy-start(f32[2048]{0:T(1024)S(1)} %get-tuple-element.14) | copy-start | bytes 24580
Sparse Core Ops, SparseCore 0:
  11.7 64.6 reduce-scatter.1
